TPU v7x, 32 devices: a whole 2x2x4 slice. The times are simulated.
32 devices in a mesh: row: 4 (over y, x), col: 8 (over z, core).
Axes of the slice: x: 2, y: 2, z: 4, core: 2. Of those that a mesh axis runs over, the one named last changes fastest.
Arguments:
- rhs: float32 [12288, 128], P('row'), may hold values from -6 to 6
- factor: float32 [10240, 4096], P('row', 'col'), may hold values from -0.09375 to 0.09375
- inverses: float32 [2, 2048, 2048], P(None, 'col', 'row'), may hold values from -1 to 3, as said below
Outputs:
- solution: float32 [4096, 128], P('col')
- remaining: float32 [8192, 128], P('row')
Inputs may be any that keep to these rules, and one draw needn't show every extreme that they name: Each inverses[k] is lower triangular in panel order with positive diagonal entries.
All inputs are finite; a program needn't handle non-finite values.
Results may differ from a plain program's by a relative error of at most 0.000068.
Values sent between devices are 32-bit elements; how exact they have to be, the bound alone decides.
A program may use at most 64 MiB of HBM per device.

v0:
```python
import jax
import jax.numpy as jnp
from jax import lax
from jax.sharding import PartitionSpec as P


def product(left, right):
    return jnp.dot(left, right, precision=lax.Precision.HIGHEST, preferred_element_type=jnp.float32)


def local(rhs, factor, inverses):
    span_rows = inverses.shape[2]
    span_cols = factor.shape[1] // 2
    first_rhs = rhs[:span_rows]
    second_rhs = rhs[span_rows : 2 * span_rows]
    trailing = rhs[2 * span_rows :]
    first_sol = lax.psum(product(inverses[0], first_rhs), "row")
    reduced = second_rhs - lax.psum(product(factor[:span_rows, :span_cols], first_sol), "col")
    carried = product(factor[span_rows:, :span_cols], first_sol)
    second_sol = lax.psum(product(inverses[1], reduced), "row")
    last_term = product(factor[span_rows:, span_cols:], second_sol)
    remaining = trailing - lax.psum(carried + last_term, "col")
    return (jnp.concatenate([first_sol, second_sol], 0), remaining)


def solution(mesh):
    in_specs = (P("row", None), P("row", "col"), P(None, "col", "row"))
    out_specs = (P("col", None), P("row", None))
    return jax.shard_map(local, mesh=mesh, in_specs=in_specs, out_specs=out_specs, check_vma=False)
```

profile of v0, /device:TPU:0, one launch (start us, length us, event | category | flops | bytes accessed | tf_op | source)
XLA Modules:
  0.0 233.2 jit_solution(9081232061759633755)
XLA Ops:
  7.2 0.0 copy-start.1
  7.2 0.0 all-reduce.5.cloned.1.call-start
  7.2 2.4 %fusion.5 = f32[256,128]{1,0:T(8,128)} fusion(f32[2,256,512]{2,1,0:T(8,128)} %param.5, f32[3072,128]{1,0:T(8,128)} %param.3), kind=kOutput, calls=%fused_computation.8 | convolution fusion | flops 201326592 | bytes 917504 | tf_op jit(solution)/shard_map/dot_general | solution.py:8
  9.6 0.0 all-reduce.5.cloned.1.call-update
  9.7 0.0 all-reduce.7.cloned.1.call-start
  9.7 46.7 %all-reduce.5.cloned.1.call-done = f32[256,128]{1,0:T(8,128)} async-done(((f32[256,128]{1,0:T(8,128)}), f32[256,128]{1,0:T(8,128)}) %all-reduce.5.cloned.1.call-update) | async-done | bytes 131088 | tf_op jit(solution)/shard_map/psum | solution.py:17
  56.4 0.0 copy-start
  56.4 2.4 %convolution_bitcast_fusion = f32[512,128]{1,0:T(8,128)} fusion(f32[256,128]{1,0:T(8,128)} %all-reduce.5.cloned.1.call-done, f32[2560,512]{1,0:T(8,128)} %param.4), kind=kOutput, calls=%fused_computation.5 | convolution fusion | flops 201326592 | bytes 917504 | tf_op jit(solution)/shard_map/dot_general | solution.py:8
  58.8 0.0 all-reduce.7.cloned.1.call-update
  58.9 0.0 all-reduce.9.cloned.1.call-start
  58.9 55.8 %all-reduce.7.cloned.1.call-done = f32[512,128]{1,0:T(8,128)} async-done(((f32[512,128]{1,0:T(8,128)}), f32[512,128]{1,0:T(8,128)}) %all-reduce.7.cloned.1.call-update) | async-done | bytes 262160 | tf_op jit(solution)/shard_map/psum | solution.py:18
  114.8 0.0 copy-done.1
  114.8 2.3 convolution_bitcast_fusion.1
  117.0 0.0 all-reduce.9.cloned.1.call-update
  117.0 0.0 all-reduce.11.cloned.1.call-start
  117.1 0.0 copy-done
  117.1 3.9 %fusion.2 = f32[128,2048]{1,0:T(8,128)S(1)} fusion(f32[256,128]{1,0:T(8,128)S(1)} %copy-done, f32[2560,512]{1,0:T(8,128)} %param.4), kind=kOutput, calls=%fused_computation.3 | convolution fusion | flops 805306368 | bytes 3276800 | tf_op jit(solution)/shard_map/dot_general | solution.py:8
  121.0 38.5 %all-reduce.9.cloned.1.call-done = f32[256,128]{1,0:T(8,128)} async-done(((f32[256,128]{1,0:T(8,128)}), f32[256,128]{1,0:T(8,128)}) %all-reduce.9.cloned.1.call-update) | async-done | bytes 131088 | tf_op jit(solution)/shard_map/psum | solution.py:20
  159.5 5.0 %fusion = f32[2048,128]{0,1:T(8,128)} fusion(f32[128,2048]{1,0:T(8,128)S(1)} %fusion.2, f32[256,128]{1,0:T(8,128)} %all-reduce.9.cloned.1.call-done, f32[2560,512]{1,0:T(8,128)} %param.4), kind=kOutput, calls=%fused_computation.1 | convolution fusion | flops 805568512 | bytes 4325376 | tf_op jit(solution)/shard_map/dot_general | solution.py:8
  164.5 0.0 all-reduce.11.cloned.1.call-update
  164.5 0.0 copy-start.2
  164.5 1.3 slice.29
  165.9 0.3 copy.9
  166.2 0.0 copy-done.2
  166.2 0.7 pad_maximum_fusion
  166.9 57.0 %all-reduce.11.cloned.1.call-done = f32[2048,128]{0,1:T(8,128)} async-done(((f32[2048,128]{0,1:T(8,128)}), f32[2048,128]{0,1:T(8,128)}) %all-reduce.11.cloned.1.call-update) | async-done | bytes 1048592 | tf_op jit(solution)/shard_map/psum | solution.py:22
  224.0 1.3 sub.7
  225.3 1.3 copy.7
Async XLA Ops:
  7.2 107.6 %copy-start.1 = (f32[2,256,512]{2,1,0:T(8,128)S(1)}, f32[2,256,512]{2,1,0:T(8,128)}, u32[]{:S(2)}) copy-start(f32[2,256,512]{2,1,0:T(8,128)} %param.5) | copy-start | bytes 3145732
  7.2 49.2 %all-reduce.5.cloned.1.call-start = ((), (), s32[]{:S(2)}) async-start(), calls=%async_computation | async-start | bytes 262144 | tf_op jit(solution)/shard_map/psum | solution.py:17
  9.7 105.1 %all-reduce.7.cloned.1.call-start = ((), (), s32[]{:S(2)}) async-start(), calls=%async_computation.1 | async-start | bytes 524288 | tf_op jit(solution)/shard_map/psum | solution.py:18
  56.4 60.7 %copy-start = (f32[256,128]{1,0:T(8,128)S(1)}, f32[256,128]{1,0:T(8,128)}, u32[]{:S(2)}) copy-start(f32[256,128]{1,0:T(8,128)} %all-reduce.5.cloned.1.call-done) | copy-start | bytes 393220
  58.9 100.7 %all-reduce.9.cloned.1.call-start = ((), (), s32[]{:S(2)}) async-start(), calls=%async_computation.2 | async-start | bytes 262144 | tf_op jit(solution)/shard_map/psum | solution.py:20
  117.0 106.9 %all-reduce.11.cloned.1.call-start = ((), (), s32[]{:S(2)}) async-start(), calls=%async_computation.3 | async-start | bytes 2097152 | tf_op jit(solution)/shard_map/psum | solution.py:22
  164.5 1.7 copy-start.2
Sparse Core Ops, SparseCore 0:
  11.4 44.9 all-reduce.4
  59.3 55.4 all-reduce.6
  118.2 41.2 all-reduce.8
  164.6 59.2 all-reduce.10
where the time goes:
time: 233 us
  waiting for transfers between devices  198 us (85%)
  matrix products  16 us (7%)
  between operations  13.8 us (6%)
  local copies, waits for them, and re-layouts  2.98 us (1%)
    psum x1, waiting for transfers between devices, local(): remaining = trailing - lax.psum(carried + last_term, 'col')  57 us
    psum x1, waiting for transfers between devices, local(): lax.psum(product(factor[:span_rows, :span_cols], first_sol), 'col')  55.8 us
    psum x1, waiting for transfers between devices, local(): first_sol = lax.psum(product(inverses[0], first_rhs), 'row')  46.7 us
    psum x1, waiting for transfers between devices, local(): second_sol = lax.psum(product(inverses[1], reduced), 'row')  38.5 us
    dot_general x5, matrix products, product(): jnp.dot(left, right, precision=lax.Precision.HIGHEST, preferred_element_t...  16 us
  transfers between devices with their start and end apart: 4, of which 4 were waited for; matrix products, arithmetic and copies ran while one was open for 3% of the time, Pallas kernels for 0%

commit v1 on v0

v1 whole, which is shorter than its diff:
```python
import functools

import jax
import jax.numpy as jnp
from jax import lax
from jax.experimental import pallas as pl
from jax.experimental.pallas import tpu as pltpu
from jax.sharding import PartitionSpec as P

MESH = pl.DeviceIdType.MESH


def halves(x):
    high = x.astype(jnp.bfloat16)
    return high, (x - high.astype(jnp.float32)).astype(jnp.bfloat16)


def product(left, right):
    (lh, ll), (rh, rl) = left, right
    dot = functools.partial(jnp.dot, preferred_element_type=jnp.float32)
    return dot(lh, rh) + (dot(lh, rl) + dot(ll, rh))


def kernel(n_row, n_col, n_mid, n_end, skew_mid, skew_end,
           rhs, factor, inverses, sol, rem,
           inv_v, rhs_v, coup_v, fac_v, sums, got, pair0, pair1, red,
           mid_p, mid_rr, mid_rl, mid_sr, mid_sl,
           end_p, end_rr, end_rl, end_sr, end_sl, fac_h, fac_l,
           load_sem, swap_send, swap_recv, row_send, row_recv,
           mid_send, mid_recv, end_send, end_recv):
    span_rows = inv_v.shape[2]
    span_cols = inv_v.shape[1]
    half_r = span_rows // 2
    trail = rem.shape[0]
    half_t = trail // 2
    width = fac_v.shape[2]
    coup_w = coup_v.shape[2]
    phases = n_row.bit_length() - 1
    n_z = n_col // 2
    r = lax.axis_index("row")
    c = lax.axis_index("col")
    z, k = c // 2, c % 2
    mate = z * 2 + 1 - k

    def at(row, col):
        return {"row": row, "col": col}

    loads = [
        pltpu.make_async_copy(inverses.at[0], inv_v.at[0], load_sem.at[0]),
        pltpu.make_async_copy(rhs.at[pl.ds(0, span_rows)], rhs_v.at[pl.ds(0, span_rows)], load_sem.at[1]),
        pltpu.make_async_copy(factor.at[pl.ds(pl.multiple_of(k * half_r, 8), half_r), pl.ds(0, coup_w)], coup_v.at[k], load_sem.at[2]),
        pltpu.make_async_copy(inverses.at[1], inv_v.at[1], load_sem.at[3]),
        pltpu.make_async_copy(rhs.at[pl.ds(span_rows, span_rows + trail)], rhs_v.at[pl.ds(span_rows, span_rows + trail)], load_sem.at[4]),
        pltpu.make_async_copy(factor.at[pl.ds(pl.multiple_of(span_rows + k * half_t, 8), half_t)], fac_v.at[k], load_sem.at[5]),
    ]
    for load in loads:
        load.start()

    barrier = pltpu.get_barrier_semaphore()
    for p in range(phases):
        pl.semaphore_signal(barrier, inc=1, device_id=at(r ^ (1 << p), c), device_id_type=MESH)
    pl.semaphore_signal(barrier, inc=1, device_id=at(r, mate), device_id_type=MESH)

    @pl.when(z > 0)
    def _():
        pl.semaphore_signal(barrier, inc=1, device_id=at(r, c - 2), device_id_type=MESH)

    @pl.when(z < n_z - 1)
    def _():
        pl.semaphore_signal(barrier, inc=1, device_id=at(r, c + 2), device_id_type=MESH)

    cut = span_cols // 2

    def row_copy(panel, p, side):
        bit = p if side == 0 else phases - 1 - p
        return pltpu.make_async_remote_copy(
            src_ref=sums.at[panel, p, side], dst_ref=got.at[panel, p, side],
            send_sem=row_send.at[panel, p, side], recv_sem=row_recv.at[panel, p, side],
            device_id=at(r ^ (1 << bit), c), device_id_type=MESH)

    def row_finish(panel, pair, first_gap, later_gap):
        for p in range(phases):
            if p == 0:
                first_gap()
            elif p == 1:
                later_gap()
            for side in range(2):
                row_copy(panel, p, side).wait_recv()
                total = sums[panel, p, side] + got[panel, p, side]
                if p < phases - 1:
                    sums[panel, p + 1, side] = total
                    row_copy(panel, p + 1, side).start()
                else:
                    pair[k, pl.ds(side * cut, cut)] = total
                    sol[pl.ds(panel * span_cols + side * cut, cut)] = total

    def swap(i, src, dst):
        return pltpu.make_async_remote_copy(
            src_ref=src, dst_ref=dst, send_sem=swap_send.at[i], recv_sem=swap_recv.at[i],
            device_id=at(r, mate), device_id_type=MESH)

    def swap_coup():
        return swap(0, factor.at[pl.ds(pl.multiple_of((1 - k) * half_r, 8), half_r), pl.ds(0, coup_w)], coup_v.at[k])

    def swap_fac():
        return swap(1, factor.at[pl.ds(pl.multiple_of(span_rows + (1 - k) * half_t, 8), half_t)], fac_v.at[k])

    def swap_pair(i, pair):
        return swap(i, pair.at[k], pair.at[k])

    class Chain:
        def __init__(self, n, skew, part, rr, rl, sr, sl, send, recv, base, out):
            self.n, self.skew, self.part, self.rr, self.rl, self.sr, self.sl = n, skew, part, rr, rl, sr, sl
            self.send, self.recv, self.base, self.out = send, recv, base, out
            self.rows = part.shape[1]

        def copy(self, way, j, src):
            dst = self.rr if way == 0 else self.rl
            return pltpu.make_async_remote_copy(
                src_ref=src.at[j], dst_ref=dst.at[j], send_sem=self.send.at[way, j], recv_sem=self.recv.at[way, j],
                device_id=at(r, c + 2 if way == 0 else c - 2), device_id_type=MESH)

        def place(self, j, core):
            return pl.ds(pl.multiple_of((core * self.n + j) * self.rows, 8), self.rows)

        def cross(self, j):
            where = self.place(j, k)
            return pltpu.make_async_remote_copy(
                src_ref=self.out.at[where], dst_ref=self.out.at[where],
                send_sem=self.send.at[2, j], recv_sem=self.recv.at[2, j],
                device_id=at(r, mate), device_id_type=MESH)

        def launch(self, j):
            @pl.when(z == 0)
            def _():
                self.copy(0, j, self.part).start()

            @pl.when(z == n_z - 1)
            def _():
                self.copy(1, j, self.part).start()

        def run(self):
            inner = (z > 0) & (z < n_z - 1)
            off_r = jnp.where(inner, jnp.maximum(0, self.skew * (2 * z - n_z + 1)), 0)
            off_l = jnp.where(inner, jnp.maximum(0, self.skew * (n_z - 1 - 2 * z)), 0)
            off_f = jnp.maximum(off_r, off_l)

            def step(t, carry):
                jr, jl, jf = t - off_r, t - off_l, t - off_f

                @pl.when((z > 0) & (jr >= 0) & (jr < self.n))
                def _():
                    self.copy(0, jr, self.sr).wait_recv()
                    self.sr[jr] = self.rr[jr] + self.part[jr]

                    @pl.when(z < n_z - 1)
                    def _():
                        self.copy(0, jr, self.sr).start()

                @pl.when((z < n_z - 1) & (jl >= 0) & (jl < self.n))
                def _():
                    self.copy(1, jl, self.sl).wait_recv()
                    self.sl[jl] = self.rl[jl] + self.part[jl]

                    @pl.when(z > 0)
                    def _():
                        self.copy(1, jl, self.sl).start()

                @pl.when((jf >= 0) & (jf < self.n))
                def _():
                    first = rhs_v[pl.ds(pl.multiple_of(self.base + (k * self.n + jf) * self.rows, 8), self.rows)]
                    where = self.place(jf, k)

                    @pl.when(z == 0)
                    def _():
                        self.out[where] = first - self.sl[jf]

                    @pl.when(z == n_z - 1)
                    def _():
                        self.out[where] = first - self.sr[jf]

                    @pl.when(inner)
                    def _():
                        self.out[where] = first - (self.sr[jf] + self.rl[jf])

                    self.cross(jf).start()

                return carry

            lax.fori_loop(0, self.n + self.skew * max(n_z - 3, 0), step, 0)

            def gather(j, carry):
                self.cross(j).wait_recv()
                return carry

            lax.fori_loop(0, self.n, gather, 0)

        def drain(self):
            def step(j, carry):
                self.cross(j).wait_send()

                @pl.when(z < n_z - 1)
                def _():
                    self.copy(0, j, self.sr).wait_send()

                @pl.when(z > 0)
                def _():
                    self.copy(1, j, self.sl).wait_send()

                return carry

            lax.fori_loop(0, self.n, step, 0)

    mid = Chain(n_mid, skew_mid, mid_p, mid_rr, mid_rl, mid_sr, mid_sl, mid_send, mid_recv, span_rows, red)
    end = Chain(n_end, skew_end, end_p, end_rr, end_rl, end_sr, end_sl, end_send, end_recv, 2 * span_rows, rem)

    loads[0].wait()
    loads[1].wait()
    right = halves(rhs_v[pl.ds(0, span_rows)])
    for side in range(2):
        sums[0, 0, side] = product(halves(inv_v[0, pl.ds(side * cut, cut)]), right)
    pl.semaphore_wait(barrier, phases + 1 + (z > 0).astype(jnp.int32) + (z < n_z - 1).astype(jnp.int32))
    for side in range(2):
        row_copy(0, 0, side).start()

    def nothing():
        pass

    row_finish(0, pair0, lambda: swap_coup().start(), nothing)
    swap_pair(2, pair0).start()

    loads[2].wait()
    swap_coup().wait_recv()
    swap_pair(2, pair0).wait_recv()
    both0 = [halves(pair0[i]) for i in range(2)]
    for j in range(n_mid):
        rows = pl.ds(j * mid.rows, mid.rows)
        mid_p[j] = product(halves(coup_v[0, rows, :span_cols]), both0[0]) + product(halves(coup_v[1, rows, :span_cols]), both0[1])
        mid.launch(j)
    loads[3].wait()
    loads[4].wait()
    loads[5].wait()
    swap_fac().start()
    mid.run()

    right = halves(red[...])
    for side in range(2):
        sums[1, 0, side] = product(halves(inv_v[1, pl.ds(side * cut, cut)]), right)
        row_copy(1, 0, side).start()

    def carried():
        swap_fac().wait_recv()

        def step(j, carry):
            rows = pl.ds(pl.multiple_of(j * end.rows, 8), end.rows)
            end_p[j] = (product(halves(fac_v[0, rows, :span_cols]), halves(pair0[0]))
                        + product(halves(fac_v[1, rows, :span_cols]), halves(pair0[1])))
            return carry

        lax.fori_loop(0, n_end, step, 0)

    def split():
        def step(j, carry):
            rows = pl.ds(pl.multiple_of(j * end.rows, 16), end.rows)
            for i in range(2):
                fac_h[i, rows], fac_l[i, rows] = halves(fac_v[i, rows, span_cols:])
            return carry

        lax.fori_loop(0, n_end, step, 0)

    row_finish(1, pair1, carried, split)
    swap_pair(3, pair1).start()
    swap_pair(3, pair1).wait_recv()

    both1 = [halves(pair1[i]) for i in range(2)]

    def last(j, carry):
        rows = pl.ds(pl.multiple_of(j * end.rows, 16), end.rows)
        end_p[j] = end_p[j] + (product((fac_h[0, rows], fac_l[0, rows]), both1[0])
                               + product((fac_h[1, rows], fac_l[1, rows]), both1[1]))
        end.launch(j)
        return carry

    lax.fori_loop(0, n_end, last, 0)
    end.run()

    mid.drain()
    end.drain()
    swap_coup().wait_send()
    swap_fac().wait_send()
    swap_pair(2, pair0).wait_send()
    swap_pair(3, pair1).wait_send()
    for panel in range(2):
        for p in range(phases):
            for side in range(2):
                row_copy(panel, p, side).wait_send()


def local(n_row, n_col, rhs, factor, inverses):
    span_cols, span_rows = inverses.shape[1:]
    width = factor.shape[1]
    dens = rhs.shape[1]
    trail = rhs.shape[0] - 2 * span_rows
    phases = n_row.bit_length() - 1
    half_r, half_t = span_rows // 2, trail // 2
    coup_w = min(width, -(-span_cols // 128) * 128)
    n_mid = min(8, half_r // 8)
    n_end = min(16, half_t // 16)
    f32 = jnp.float32

    def chain_bufs(n, half):
        return [pltpu.VMEM((n, half // n, dens), f32)] * 5

    scratch = [
        pltpu.VMEM(inverses.shape, f32),
        pltpu.VMEM(rhs.shape, f32),
        pltpu.VMEM((2, half_r, coup_w), f32),
        pltpu.VMEM((2, half_t, width), f32),
        pltpu.VMEM((2, phases, 2, span_cols // 2, dens), f32),
        pltpu.VMEM((2, phases, 2, span_cols // 2, dens), f32),
        pltpu.VMEM((2, span_cols, dens), f32),
        pltpu.VMEM((2, span_cols, dens), f32),
        pltpu.VMEM((span_rows, dens), f32),
        *chain_bufs(n_mid, half_r),
        *chain_bufs(n_end, half_t),
        pltpu.VMEM((2, half_t, span_cols), jnp.bfloat16),
        pltpu.VMEM((2, half_t, span_cols), jnp.bfloat16),
        pltpu.SemaphoreType.DMA((6,)),
        pltpu.SemaphoreType.DMA((4,)),
        pltpu.SemaphoreType.DMA((4,)),
        pltpu.SemaphoreType.DMA((2, phases, 2)),
        pltpu.SemaphoreType.DMA((2, phases, 2)),
        pltpu.SemaphoreType.DMA((3, n_mid)),
        pltpu.SemaphoreType.DMA((3, n_mid)),
        pltpu.SemaphoreType.DMA((3, n_end)),
        pltpu.SemaphoreType.DMA((3, n_end)),
    ]
    return pl.pallas_call(
        functools.partial(kernel, n_row, n_col, n_mid, n_end, 4, 3),
        out_shape=(jax.ShapeDtypeStruct((2 * span_cols, dens), f32), jax.ShapeDtypeStruct((trail, dens), f32)),
        in_specs=[pl.BlockSpec(memory_space=pl.ANY)] * 3,
        out_specs=(pl.BlockSpec(memory_space=pltpu.VMEM), pl.BlockSpec(memory_space=pltpu.VMEM)),
        scratch_shapes=scratch,
        compiler_params=pltpu.CompilerParams(collective_id=0, has_side_effects=True),
    )(rhs, factor, inverses)


def solution(mesh):
    in_specs = (P("row", None), P("row", "col"), P(None, "col", "row"))
    out_specs = (P("col", None), P("row", None))
    body = functools.partial(local, mesh.shape["row"], mesh.shape["col"])
    return jax.shard_map(body, mesh=mesh, in_specs=in_specs, out_specs=out_specs, check_vma=False)
```

time: 233 us -> 63.1 us (0.27)
  waiting for transfers between devices: 198 us -> 0 us
  Pallas kernels: 0 us -> 58.3 us
  matrix products: 16 us -> 0 us
  between operations: 13.8 us -> 0.64 us
    psum x4 -> x0, waiting for transfers between devices: 198 us -> none  [the longest x1 57 us: local(): remaining = trailing - lax.psum(carried + last_term, 'col')]
    pallas_call x0 -> x1, Pallas kernels: none -> 58.3 us  [local(): pl.pallas_call(functools.partial(kernel, n_row, n_col, n_mid, n_end, 4, 3...]
    dot_general x5 -> x0, matrix products: 16 us -> none  [product(): jnp.dot(left, right, precision=lax.Precision.HIGHEST, preferred_element_t...]
  transfers between devices with their start and end apart: 4 -> 0, of which waited for: 4 -> 0; matrix products, arithmetic and copies ran while one was open for 3% -> 0% of each run, Pallas kernels for 0% -> 0%
where the time goes in v1:
time: 63.1 us; the launch traced here: 62.9 us
  Pallas kernels  58.3 us (92%)
  local copies, waits for them, and re-layouts  3.93 us (6%)
  between operations  0.64 us (1%)
    pallas_call x1, Pallas kernels, local(): pl.pallas_call(functools.partial(kernel, n_row, n_col, n_mid, n_end, 4, 3...  58.3 us
    unnamed x2, local copies, waits for them, and re-layouts  3.93 us

profile of v1, /device:TPU:0, one launch (start us, length us, event | category | flops | bytes accessed | tf_op | source)
XLA Modules:
  0.0 62.9 jit_solution(5440482496805067354)
XLA Ops:
  0.6 58.3 %shard_map.50 = (f32[512,128]{1,0:T(8,128)}, f32[2048,128]{1,0:T(8,128)}) custom-call(f32[3072,128]{1,0:T(8,128)} %rhs.1, f32[2560,512]{1,0:T(8,128)} %factor.1, f32[2,256,512]{2,1,0:T(8,128)} %inverses.1), custom_call_target="tpu_custom_call" | custom-call | tf_op jit(solution)/shard_map/pallas_call | solution.py:338
  58.9 1.7 %copy.7 = f32[512,128]{1,0:T(8,128)} copy(f32[512,128]{1,0:T(8,128)} %get-tuple-element.4) | data formatting | bytes 524288
  60.6 2.3 %copy.8 = f32[2048,128]{1,0:T(8,128)} copy(f32[2048,128]{1,0:T(8,128)} %get-tuple-element.5) | data formatting | bytes 2097152

commit v2 on v1

--- a/solution.py
+++ b/solution.py
@@ -53,7 +53,7 @@
         pltpu.make_async_copy(rhs.at[pl.ds(span_rows, span_rows + trail)], rhs_v.at[pl.ds(span_rows, span_rows + trail)], load_sem.at[4]),
         pltpu.make_async_copy(factor.at[pl.ds(pl.multiple_of(span_rows + k * half_t, 8), half_t)], fac_v.at[k], load_sem.at[5]),
     ]
-    for load in loads:
+    for load in loads[:2]:
         load.start()
 
     barrier = pltpu.get_barrier_semaphore()
@@ -69,10 +69,11 @@
     def _():
         pl.semaphore_signal(barrier, inc=1, device_id=at(r, c + 2), device_id_type=MESH)
 
-    cut = span_cols // 2
+    pieces = sums.shape[2]
+    cut = span_cols // pieces
 
     def row_copy(panel, p, side):
-        bit = p if side == 0 else phases - 1 - p
+        bit = p if side % 2 == 0 else phases - 1 - p
         return pltpu.make_async_remote_copy(
             src_ref=sums.at[panel, p, side], dst_ref=got.at[panel, p, side],
             send_sem=row_send.at[panel, p, side], recv_sem=row_recv.at[panel, p, side],
@@ -84,7 +85,7 @@
                 first_gap()
             elif p == 1:
                 later_gap()
-            for side in range(2):
+            for side in range(pieces):
                 row_copy(panel, p, side).wait_recv()
                 total = sums[panel, p, side] + got[panel, p, side]
                 if p < phases - 1:
@@ -216,11 +217,13 @@
 
     loads[0].wait()
     loads[1].wait()
+    for load in loads[2:]:
+        load.start()
     right = halves(rhs_v[pl.ds(0, span_rows)])
-    for side in range(2):
+    for side in range(pieces):
         sums[0, 0, side] = product(halves(inv_v[0, pl.ds(side * cut, cut)]), right)
     pl.semaphore_wait(barrier, phases + 1 + (z > 0).astype(jnp.int32) + (z < n_z - 1).astype(jnp.int32))
-    for side in range(2):
+    for side in range(pieces):
         row_copy(0, 0, side).start()
 
     def nothing():
@@ -244,7 +247,7 @@
     mid.run()
 
     right = halves(red[...])
-    for side in range(2):
+    for side in range(pieces):
         sums[1, 0, side] = product(halves(inv_v[1, pl.ds(side * cut, cut)]), right)
         row_copy(1, 0, side).start()
 
@@ -292,7 +295,7 @@
     swap_pair(3, pair1).wait_send()
     for panel in range(2):
         for p in range(phases):
-            for side in range(2):
+            for side in range(pieces):
                 row_copy(panel, p, side).wait_send()
 
 
@@ -305,7 +308,8 @@
     half_r, half_t = span_rows // 2, trail // 2
     coup_w = min(width, -(-span_cols // 128) * 128)
     n_mid = min(8, half_r // 8)
-    n_end = min(16, half_t // 16)
+    n_end = min(8, half_t // 16)
+    pieces = 4
     f32 = jnp.float32
 
     def chain_bufs(n, half):
@@ -316,8 +320,8 @@
         pltpu.VMEM(rhs.shape, f32),
         pltpu.VMEM((2, half_r, coup_w), f32),
         pltpu.VMEM((2, half_t, width), f32),
-        pltpu.VMEM((2, phases, 2, span_cols // 2, dens), f32),
-        pltpu.VMEM((2, phases, 2, span_cols // 2, dens), f32),
+        pltpu.VMEM((2, phases, pieces, span_cols // pieces, dens), f32),
+        pltpu.VMEM((2, phases, pieces, span_cols // pieces, dens), f32),
         pltpu.VMEM((2, span_cols, dens), f32),
         pltpu.VMEM((2, span_cols, dens), f32),
         pltpu.VMEM((span_rows, dens), f32),
@@ -328,16 +332,16 @@
         pltpu.SemaphoreType.DMA((6,)),
         pltpu.SemaphoreType.DMA((4,)),
         pltpu.SemaphoreType.DMA((4,)),
-        pltpu.SemaphoreType.DMA((2, phases, 2)),
-        pltpu.SemaphoreType.DMA((2, phases, 2)),
+        pltpu.SemaphoreType.DMA((2, phases, pieces)),
+        pltpu.SemaphoreType.DMA((2, phases, pieces)),
         pltpu.SemaphoreType.DMA((3, n_mid)),
         pltpu.SemaphoreType.DMA((3, n_mid)),
         pltpu.SemaphoreType.DMA((3, n_end)),
         pltpu.SemaphoreType.DMA((3, n_end)),
     ]
     return pl.pallas_call(
-        functools.partial(kernel, n_row, n_col, n_mid, n_end, 4, 3),
-        out_shape=(jax.ShapeDtypeStruct((2 * span_cols, dens), f32), jax.ShapeDtypeStruct((trail, dens), f32)),
+        functools.partial(kernel, n_row, n_col, n_mid, n_end, 5, 2),
+        out_shape=(pltpu.VMEM((2 * span_cols, dens), f32), pltpu.VMEM((trail, dens), f32)),
         in_specs=[pl.BlockSpec(memory_space=pl.ANY)] * 3,
         out_specs=(pl.BlockSpec(memory_space=pltpu.VMEM), pl.BlockSpec(memory_space=pltpu.VMEM)),
         scratch_shapes=scratch,

time: 63.1 us -> 57 us (0.903)
  Pallas kernels: 58.3 us -> 54.6 us
  local copies, waits for them, and re-layouts: 3.93 us -> 1.67 us
    pallas_call x1, Pallas kernels: 58.3 us -> 54.6 us  [local(): pl.pallas_call(functools.partial(kernel, n_row, n_col, n_mid, n_end, 5, 2...]
    unnamed x2, local copies, waits for them, and re-layouts: 3.93 us -> 1.67 us
where the time goes in v2:
time: 57 us; the launch traced here: 56.9 us
  Pallas kernels  54.6 us (96%)
  local copies, waits for them, and re-layouts  1.67 us (3%)
  between operations  0.64 us (1%)
    pallas_call x1, Pallas kernels, local(): pl.pallas_call(functools.partial(kernel, n_row, n_col, n_mid, n_end, 5, 2...  54.6 us
    unnamed x2, local copies, waits for them, and re-layouts  1.67 us

profile of v2, /device:TPU:0, one launch (start us, length us, event | category | flops | bytes accessed | tf_op | source)
XLA Modules:
  0.0 56.9 jit_solution(5448911908009622270)
XLA Ops:
  0.6 54.6 %shard_map.50 = (f32[512,128]{1,0:T(8,128)S(1)}, f32[2048,128]{1,0:T(8,128)S(1)}) custom-call(f32[3072,128]{1,0:T(8,128)} %rhs.1, f32[2560,512]{1,0:T(8,128)} %factor.1, f32[2,256,512]{2,1,0:T(8,128)} %inverses.1), custom_call_target="tpu_custom_call" | custom-call | tf_op jit(solution)/shard_map/pallas_call | solution.py:342
  55.2 0.7 %copy.7 = f32[512,128]{1,0:T(8,128)} copy(f32[512,128]{1,0:T(8,128)S(1)} %get-tuple-element.2) | data formatting | bytes 524288
  55.9 1.0 %copy.8 = f32[2048,128]{1,0:T(8,128)} copy(f32[2048,128]{1,0:T(8,128)S(1)} %get-tuple-element.3) | data formatting | bytes 2097152

commit v3 on v2

--- a/solution.py
+++ b/solution.py
@@ -220,8 +220,9 @@
     for load in loads[2:]:
         load.start()
     right = halves(rhs_v[pl.ds(0, span_rows)])
+    total = product(halves(inv_v[0]), right)
     for side in range(pieces):
-        sums[0, 0, side] = product(halves(inv_v[0, pl.ds(side * cut, cut)]), right)
+        sums[0, 0, side] = total[side * cut:(side + 1) * cut]
     pl.semaphore_wait(barrier, phases + 1 + (z > 0).astype(jnp.int32) + (z < n_z - 1).astype(jnp.int32))
     for side in range(pieces):
         row_copy(0, 0, side).start()
@@ -236,9 +237,9 @@
     swap_coup().wait_recv()
     swap_pair(2, pair0).wait_recv()
     both0 = [halves(pair0[i]) for i in range(2)]
+    total = product(halves(coup_v[0, :, :span_cols]), both0[0]) + product(halves(coup_v[1, :, :span_cols]), both0[1])
     for j in range(n_mid):
-        rows = pl.ds(j * mid.rows, mid.rows)
-        mid_p[j] = product(halves(coup_v[0, rows, :span_cols]), both0[0]) + product(halves(coup_v[1, rows, :span_cols]), both0[1])
+        mid_p[j] = total[j * mid.rows:(j + 1) * mid.rows]
         mid.launch(j)
     loads[3].wait()
     loads[4].wait()
@@ -247,8 +248,9 @@
     mid.run()
 
     right = halves(red[...])
+    total = product(halves(inv_v[1]), right)
     for side in range(pieces):
-        sums[1, 0, side] = product(halves(inv_v[1, pl.ds(side * cut, cut)]), right)
+        sums[1, 0, side] = total[side * cut:(side + 1) * cut]
         row_copy(1, 0, side).start()
 
     def carried():
@@ -277,14 +279,18 @@
 
     both1 = [halves(pair1[i]) for i in range(2)]
 
+    group = max(1, n_end // 4)
+
     def last(j, carry):
-        rows = pl.ds(pl.multiple_of(j * end.rows, 16), end.rows)
-        end_p[j] = end_p[j] + (product((fac_h[0, rows], fac_l[0, rows]), both1[0])
-                               + product((fac_h[1, rows], fac_l[1, rows]), both1[1]))
-        end.launch(j)
+        rows = pl.ds(pl.multiple_of(j * group * end.rows, 16), group * end.rows)
+        total = (product((fac_h[0, rows], fac_l[0, rows]), both1[0])
+                 + product((fac_h[1, rows], fac_l[1, rows]), both1[1]))
+        for i in range(group):
+            end_p[j * group + i] = end_p[j * group + i] + total[i * end.rows:(i + 1) * end.rows]
+            end.launch(j * group + i)
         return carry
 
-    lax.fori_loop(0, n_end, last, 0)
+    lax.fori_loop(0, n_end // group, last, 0)
     end.run()
 
     mid.drain()
@@ -307,8 +313,8 @@
     phases = n_row.bit_length() - 1
     half_r, half_t = span_rows // 2, trail // 2
     coup_w = min(width, -(-span_cols // 128) * 128)
-    n_mid = min(8, half_r // 8)
-    n_end = min(8, half_t // 16)
+    n_mid = min(4, half_r // 8)
+    n_end = min(16, half_t // 16)
     pieces = 4
     f32 = jnp.float32
 
@@ -340,7 +346,7 @@
         pltpu.SemaphoreType.DMA((3, n_end)),
     ]
     return pl.pallas_call(
-        functools.partial(kernel, n_row, n_col, n_mid, n_end, 5, 2),
+        functools.partial(kernel, n_row, n_col, n_mid, n_end, 3, 4),
         out_shape=(pltpu.VMEM((2 * span_cols, dens), f32), pltpu.VMEM((trail, dens), f32)),
         in_specs=[pl.BlockSpec(memory_space=pl.ANY)] * 3,
         out_specs=(pl.BlockSpec(memory_space=pltpu.VMEM), pl.BlockSpec(memory_space=pltpu.VMEM)),

time: 57 us -> 56.6 us (level)
  no operation moved by 1% of the time
where the time goes in v3:
time: 56.6 us; the launch traced here: 56.4 us
  Pallas kernels  54.1 us (96%)
  local copies, waits for them, and re-layouts  1.67 us (3%)
  between operations  0.64 us (1%)
    pallas_call x1, Pallas kernels, local(): pl.pallas_call(functools.partial(kernel, n_row, n_col, n_mid, n_end, 3, 4...  54.1 us
    unnamed x2, local copies, waits for them, and re-layouts  1.67 us

profile of v3, /device:TPU:0, one launch (start us, length us, event | category | flops | bytes accessed | tf_op | source)
XLA Modules:
  0.0 56.4 jit_solution(13776025662647046008)
XLA Ops:
  0.6 54.1 %shard_map.50 = (f32[512,128]{1,0:T(8,128)S(1)}, f32[2048,128]{1,0:T(8,128)S(1)}) custom-call(f32[3072,128]{1,0:T(8,128)} %rhs.1, f32[2560,512]{1,0:T(8,128)} %factor.1, f32[2,256,512]{2,1,0:T(8,128)} %inverses.1), custom_call_target="tpu_custom_call" | custom-call | tf_op jit(solution)/shard_map/pallas_call | solution.py:348
  54.8 0.7 %copy.7 = f32[512,128]{1,0:T(8,128)} copy(f32[512,128]{1,0:T(8,128)S(1)} %get-tuple-element.2) | data formatting | bytes 524288
  55.5 1.0 %copy.8 = f32[2048,128]{1,0:T(8,128)} copy(f32[2048,128]{1,0:T(8,128)S(1)} %get-tuple-element.3) | data formatting | bytes 2097152
